TPU v7x, 256 devices: a whole 4x4x8 slice. The times are simulated.
256 devices in a mesh: bank: 64 (over z, y, core), zero: 4 (over x).
Axes of the slice: x: 4, y: 4, z: 8, core: 2. Of those that a mesh axis runs over, the one named last changes fastest.
Arguments:
- train_down: float32 [128, 768, 2048], P('bank', None, 'zero'), may hold values from -0.3125 to 0.3125
- other_down: float32 [128, 768, 2048], P('bank', None, 'zero'), may hold values from -0.21875 to 0.21875
- router_weight: float32 [2048, 128], P('zero', 'bank'), may hold values from -0.125 to 0.125
- router_gain: float32 [2048], P('zero'), may hold values from 0.25 to 1.75
Outputs:
- ready_down: bfloat16 [128, 768, 2048], P('bank')
- scale_down: float32 [128, 768], P('bank')
- serve_router: bfloat16 [2048, 128], replicated
- latest_down: float32 [128, 768, 2048], P('bank', None, 'zero')
All inputs are finite; a program needn't handle non-finite values. Where the computation divides by a largest or mean magnitude, that divisor is 1e-20 or more.
Results may differ from a plain program's by a relative error of at most 0.001.
Values may be sent and summed in bfloat16 or wider, within the bound.
A program may use at most 128 MiB of HBM per device.

v0:
```python
import jax
import jax.numpy as jnp
from jax import lax
from jax.sharding import Mesh
from jax.sharding import PartitionSpec as P

D_MODEL = 2048
BANK = ("bank_0", "bank_1", "bank_2")


def copy_for_each(x, axis):
    devices = lax.axis_size(axis)
    return lax.all_to_all(jnp.broadcast_to(x[None], (devices, *x.shape)), axis, 0, 0, tiled=True)


def of_everyone(x, axis):
    return copy_for_each(x, axis).sum(axis=0)


def in_order(blocks, dim):
    blocks = jnp.moveaxis(blocks, 0, dim)
    shape = blocks.shape
    return blocks.reshape(*shape[:dim], shape[dim] * shape[dim + 1], *shape[dim + 2 :])


def all_blocks(x, axes, turns):
    blocks = x
    for k in turns:
        blocks = lax.all_gather(blocks, axes[k])
    done = turns[::-1]
    back = [done.index(k) for k in range(len(axes))]
    blocks = blocks.transpose(*back, *range(len(axes), blocks.ndim))
    return blocks.reshape(-1, *x.shape)


def gather_axes(x, axes, turns, dim):
    return in_order(all_blocks(x, axes, turns), dim)


def shards(train_down, other_down, router_weight, router_gain):
    latest_down = 0.5 * other_down + 0.5 * train_down
    total_down = of_everyone(jnp.sum(jnp.abs(latest_down), axis=2), "zero")
    scale_down = total_down / D_MODEL
    narrow_down = (latest_down / jnp.expand_dims(scale_down, 2)).astype(jnp.bfloat16)
    ready_down = lax.all_gather(narrow_down, "zero", axis=2, tiled=True)
    part_router = (router_weight * router_gain[:, None]).astype(jnp.bfloat16)
    row_router = lax.all_gather(part_router, "zero", axis=0, tiled=True)
    serve_router = gather_axes(row_router, BANK, (1, 0, 2), 1)
    return (ready_down, scale_down, serve_router, latest_down)


def solution(mesh):
    split = Mesh(
        mesh.devices.reshape(8, 4, 2, mesh.shape["zero"]), ("bank_0", "bank_1", "bank_2", "zero")
    )
    placed = (P(BANK, None, "zero"), P(BANK, None, "zero"), P("zero", BANK), P("zero"))
    return jax.shard_map(
        shards,
        mesh=split,
        in_specs=placed,
        out_specs=(P(BANK, None, None), P(BANK, None), P(), P(BANK, None, "zero")),
        check_vma=False,
    )
```

profile of v0, /device:TPU:1, one launch (start us, length us, event | category | flops | bytes accessed | tf_op | source)
XLA Modules:
  0.0 105.1 jit_solution(9432049307572382526)
XLA Ops:
  7.2 0.0 all-gather.5.cloned.1.call-start
  7.2 3.3 %abs_reduce_fusion = (f32[2,768]{1,0:T(2,128)S(1)}, f32[2,768,512]{2,1,0:T(8,128)S(1)}) fusion(f32[2,768,512]{2,1,0:T(8,128)} %param.5, f32[2,768,512]{2,1,0:T(8,128)} %param.4), kind=kLoop, calls=%fused_computation.1 | loop fusion | flops 3144192 | bytes 9443328 | tf_op jit(solution)/shard_map/reduce_sum | solution.py:42
  10.6 0.0 copy-start
  10.6 8.9 %all_to_all.5 = f32[4,2,768]{2,1,0:T(2,128)S(1)} all-to-all(f32[4,2,768]{2,1,0:T(2,128)S(1)} %broadcast_in_dim.2), channel_id=1, replica_groups=mesh['bank_0'=8,'bank_1'=4,'bank_2'=2,'zero'=4] {'zero'}, dimensions={0} | all-to-all | bytes 49152 | tf_op jit(solution)/shard_map/all_to_all | solution.py:13
  19.5 0.0 copy-start.1
  19.5 0.0 copy-start.2
  19.5 0.0 copy-start.3
  19.5 1.4 %divide_convert_fusion = bf16[2,768,512]{2,1,0:T(8,128)(2,1)} fusion(f32[2,768,512]{2,1,0:T(8,128)S(1)} %get-tuple-element.33, f32[2,768]{1,0:T(2,128)S(1)} %broadcast_multiply_fusion), kind=kLoop, calls=%fused_computation | loop fusion | flops 1572864 | bytes 4724736 | tf_op jit(solution)/shard_map/convert_element_type | solution.py:44
  21.0 0.0 all-gather.5.cloned.1.call-update
  21.0 0.0 copy-done
  21.0 0.0 copy-done.1
  21.0 0.0 copy-done.2
  21.0 0.0 copy-done.3
  21.1 8.1 %all_gather.25 = bf16[2048,2]{0,1:T(2,128)(2,1)S(1)} all-gather(bf16[512,2]{0,1:T(2,128)(2,1)S(1)} %multiply_convert_fusion), channel_id=1, replica_groups=mesh['bank_0'=8,'bank_1'=4,'bank_2'=2,'zero'=4] {'zero'}, dimensions={0}, use_global_device_ids=true | all-gather | bytes 10240 | tf_op jit(solution)/shard_map/all_gather | solution.py:47
  29.2 9.5 %all-gather = bf16[8192,2]{0,1:T(2,128)(2,1)S(1)} all-gather(bf16[2048,2]{0,1:T(2,128)(2,1)S(1)} %all_gather.25), channel_id=2, replica_groups=mesh['bank_0'=8,'bank_1'=4,'bank_2'=2,'zero'=4] {'bank_1'}, dimensions={0}, use_global_device_ids=true | all-gather | bytes 40960 | tf_op jit(solution)/shard_map/all_gather | solution.py:29
  38.7 24.8 %all-gather.1 = bf16[32,2048,2]{1,2,0:T(2,128)(2,1)S(1)} all-gather(bf16[4,2048,2]{1,2,0:T(2,128)(2,1)S(1)} %bitcast.15), channel_id=3, replica_groups=mesh['bank_0'=8,'bank_1'=4,'bank_2'=2,'zero'=4] {'bank_0'}, dimensions={0}, use_global_device_ids=true | all-gather | bytes 294912 | tf_op jit(solution)/shard_map/all_gather | solution.py:29
  63.6 0.1 copy.22
  63.7 12.7 %all-gather.2 = bf16[16,4,2048,2]{2,1,3,0:T(4,128)(2,1)S(1)} all-gather(bf16[8,4,2048,2]{2,1,3,0:T(4,128)(2,1)S(1)} %copy.22), channel_id=4, replica_groups=mesh['bank_0'=8,'bank_1'=4,'bank_2'=2,'zero'=4] {'bank_2'}, dimensions={0}, use_global_device_ids=true | all-gather | bytes 786432 | tf_op jit(solution)/shard_map/all_gather | solution.py:29
  76.5 0.3 copy.28
  76.7 0.5 copy.24
  77.3 0.2 reshape.20
  77.5 1.0 copy.25
  78.5 13.2 %all-gather.5.cloned.1.call-done = bf16[2,768,2048]{2,1,0:T(8,128)(2,1)} async-done(((bf16[2,768,512]{2,1,0:T(8,128)(2,1)}), bf16[2,768,2048]{2,1,0:T(8,128)(2,1)}) %all-gather.5.cloned.1.call-update) | async-done | bytes 6291472 | tf_op jit(solution)/shard_map/all_gather | solution.py:45
  91.7 6.6 %copy.30 = bf16[2,768,2048]{2,1,0:T(8,128)(2,1)} copy(bf16[2,768,2048]{2,1,0:T(8,128)(2,1)} %all-gather.5.cloned.1.call-done) | data formatting | bytes 12582912
  (4 shorter events, 0.0 us)
Async XLA Ops:
  7.2 84.5 %all-gather.5.cloned.1.call-start = ((), (), s32[]{:S(2)}) async-start(), calls=%async_computation.1 | async-start | bytes 7864320 | tf_op jit(solution)/shard_map/all_gather | solution.py:45
  10.6 10.4 %copy-start = (f32[2,768,512]{2,1,0:T(8,128)}, f32[2,768,512]{2,1,0:T(8,128)S(1)}, u32[]{:S(2)}) copy-start(f32[2,768,512]{2,1,0:T(8,128)S(1)} %get-tuple-element.33) | copy-start | bytes 9437188
  19.5 1.5 %copy-start.1 = (f32[2,768]{1,0:T(2,128)}, f32[2,768]{1,0:T(2,128)S(1)}, u32[]{:S(2)}) copy-start(f32[2,768]{1,0:T(2,128)S(1)} %broadcast_multiply_fusion) | copy-start | bytes 18436
  19.5 1.5 %copy-start.2 = (f32[512,2]{0,1:T(2,128)S(1)}, f32[512,2]{0,1:T(2,128)}, u32[]{:S(2)}) copy-start(f32[512,2]{0,1:T(2,128)} %param.6) | copy-start | bytes 12292
  19.5 1.5 %copy-start.3 = (f32[512]{0:T(512)S(1)}, f32[512]{0:T(512)}, u32[]{:S(2)}) copy-start(f32[512]{0:T(512)} %param.7) | copy-start | bytes 6148
Sparse Core Ops, SparseCore 0:
  21.1 70.5 all-gather.4
where the time goes:
time: 105 us
  blocking collectives  64.1 us (61%)
  between operations  14.1 us (13%)
  waiting for transfers between devices  13.2 us (13%)
  local copies, waits for them, and re-layouts  8.81 us (8%)
  other arithmetic  4.81 us (5%)
    all_gather x3, blocking collectives, all_blocks(): blocks = lax.all_gather(blocks, axes[k])  47.1 us
    all_gather x1, waiting for transfers between devices, shards(): ready_down = lax.all_gather(narrow_down, 'zero', axis=2, tiled=True)  13.2 us
    all_to_all x1, blocking collectives, copy_for_each(): lax.all_to_all(jnp.broadcast_to(x[None], (devices, *x.shape)), axis, 0, 0...  8.89 us
    all_gather x1, blocking collectives, shards(): row_router = lax.all_gather(part_router, 'zero', axis=0, tiled=True)  8.14 us
    unnamed x10, local copies, waits for them, and re-layouts  7.64 us
    reduce_sum x1, other arithmetic, shards(): total_down = of_everyone(jnp.sum(jnp.abs(latest_down), axis=2), 'zero')  3.34 us
  transfers between devices with their start and end apart: 1, of which 1 were waited for; matrix products, arithmetic and copies ran while one was open for 2% of the time, Pallas kernels for 0%

commit v1 on v0

--- a/solution.py
+++ b/solution.py
@@ -42,7 +42,7 @@
     total_down = of_everyone(jnp.sum(jnp.abs(latest_down), axis=2), "zero")
     scale_down = total_down / D_MODEL
     narrow_down = (latest_down / jnp.expand_dims(scale_down, 2)).astype(jnp.bfloat16)
-    ready_down = lax.all_gather(narrow_down, "zero", axis=2, tiled=True)
+    ready_down = jnp.concatenate(lax.all_gather(narrow_down, "zero"), axis=2)
     part_router = (router_weight * router_gain[:, None]).astype(jnp.bfloat16)
     row_router = lax.all_gather(part_router, "zero", axis=0, tiled=True)
     serve_router = gather_axes(row_router, BANK, (1, 0, 2), 1)

time: 105 us -> 105 us (level)
    unnamed x10 -> x9, local copies, waits for them, and re-layouts: 7.64 us -> 1.02 us
    reshape x0 -> x1, local copies, waits for them, and re-layouts: none -> 6.47 us  [shards(): ready_down = jnp.concatenate(lax.all_gather(narrow_down, 'zero'), axis=2)]
where the time goes in v1:
time: 105 us
  blocking collectives  64.1 us (61%)
  between operations  14.1 us (13%)
  waiting for transfers between devices  13.2 us (13%)
  local copies, waits for them, and re-layouts  8.67 us (8%)
  other arithmetic  4.81 us (5%)
    all_gather x3, blocking collectives, all_blocks(): blocks = lax.all_gather(blocks, axes[k])  47.1 us
    all_gather x1, waiting for transfers between devices, shards(): ready_down = jnp.concatenate(lax.all_gather(narrow_down, 'zero'), axis=2)  13.2 us
    all_to_all x1, blocking collectives, copy_for_each(): lax.all_to_all(jnp.broadcast_to(x[None], (devices, *x.shape)), axis, 0, 0...  8.89 us
    all_gather x1, blocking collectives, shards(): row_router = lax.all_gather(part_router, 'zero', axis=0, tiled=True)  8.14 us
    reshape x1, local copies, waits for them, and re-layouts, shards(): ready_down = jnp.concatenate(lax.all_gather(narrow_down, 'zero'), axis=2)  6.47 us
    reduce_sum x1, other arithmetic, shards(): total_down = of_everyone(jnp.sum(jnp.abs(latest_down), axis=2), 'zero')  3.34 us
  transfers between devices with their start and end apart: 1, of which 1 were waited for; matrix products, arithmetic and copies ran while one was open for 2% of the time, Pallas kernels for 0%

profile of v1, /device:TPU:1, one launch (start us, length us, event | category | flops | bytes accessed | tf_op | source)
XLA Modules:
  0.0 105.0 jit_solution(14287151314433224797)
XLA Ops:
  7.2 0.0 all-gather.6.cloned.1.call-start
  7.2 3.3 %abs_reduce_fusion = (f32[2,768]{1,0:T(2,128)S(1)}, f32[2,768,512]{2,1,0:T(8,128)S(1)}) fusion(f32[2,768,512]{2,1,0:T(8,128)} %param.5, f32[2,768,512]{2,1,0:T(8,128)} %param.4), kind=kLoop, calls=%fused_computation.1 | loop fusion | flops 3144192 | bytes 9443328 | tf_op jit(solution)/shard_map/reduce_sum | solution.py:42
  10.6 0.0 copy-start
  10.6 8.9 %all_to_all.5 = f32[4,2,768]{2,1,0:T(2,128)S(1)} all-to-all(f32[4,2,768]{2,1,0:T(2,128)S(1)} %broadcast_in_dim.2), channel_id=1, replica_groups=mesh['bank_0'=8,'bank_1'=4,'bank_2'=2,'zero'=4] {'zero'}, dimensions={0} | all-to-all | bytes 49152 | tf_op jit(solution)/shard_map/all_to_all | solution.py:13
  19.5 0.0 copy-start.1
  19.5 0.0 copy-start.2
  19.5 0.0 copy-start.3
  19.5 1.4 %divide_convert_fusion = bf16[2,768,512]{2,1,0:T(8,128)(2,1)} fusion(f32[2,768,512]{2,1,0:T(8,128)S(1)} %get-tuple-element.25, f32[2,768]{1,0:T(2,128)S(1)} %broadcast_multiply_fusion), kind=kLoop, calls=%fused_computation | loop fusion | flops 1572864 | bytes 4724736 | tf_op jit(solution)/shard_map/convert_element_type | solution.py:44
  21.0 0.0 all-gather.6.cloned.1.call-update
  21.0 0.0 copy-done
  21.0 0.0 copy-done.1
  21.0 0.0 copy-done.2
  21.0 0.0 copy-done.3
  21.1 8.1 %all_gather.29 = bf16[2048,2]{0,1:T(2,128)(2,1)S(1)} all-gather(bf16[512,2]{0,1:T(2,128)(2,1)S(1)} %multiply_convert_fusion), channel_id=1, replica_groups=mesh['bank_0'=8,'bank_1'=4,'bank_2'=2,'zero'=4] {'zero'}, dimensions={0}, use_global_device_ids=true | all-gather | bytes 10240 | tf_op jit(solution)/shard_map/all_gather | solution.py:47
  29.2 9.5 %all-gather.1 = bf16[8192,2]{0,1:T(2,128)(2,1)S(1)} all-gather(bf16[2048,2]{0,1:T(2,128)(2,1)S(1)} %all_gather.29), channel_id=3, replica_groups=mesh['bank_0'=8,'bank_1'=4,'bank_2'=2,'zero'=4] {'bank_1'}, dimensions={0}, use_global_device_ids=true | all-gather | bytes 40960 | tf_op jit(solution)/shard_map/all_gather | solution.py:29
  38.7 24.8 %all-gather.2 = bf16[32,2048,2]{1,2,0:T(2,128)(2,1)S(1)} all-gather(bf16[4,2048,2]{1,2,0:T(2,128)(2,1)S(1)} %bitcast.22), channel_id=4, replica_groups=mesh['bank_0'=8,'bank_1'=4,'bank_2'=2,'zero'=4] {'bank_0'}, dimensions={0}, use_global_device_ids=true | all-gather | bytes 294912 | tf_op jit(solution)/shard_map/all_gather | solution.py:29
  63.6 0.1 copy.28
  63.7 12.7 %all-gather.3 = bf16[16,4,2048,2]{2,1,3,0:T(4,128)(2,1)S(1)} all-gather(bf16[8,4,2048,2]{2,1,3,0:T(4,128)(2,1)S(1)} %copy.28), channel_id=5, replica_groups=mesh['bank_0'=8,'bank_1'=4,'bank_2'=2,'zero'=4] {'bank_2'}, dimensions={0}, use_global_device_ids=true | all-gather | bytes 786432 | tf_op jit(solution)/shard_map/all_gather | solution.py:29
  76.5 0.3 copy.35
  76.7 0.5 copy.30
  77.3 0.2 reshape.28
  77.5 1.0 copy.31
  78.5 13.2 %all-gather.6.cloned.1.call-done = bf16[8,768,512]{2,1,0:T(8,128)(2,1)} async-done(((bf16[2,768,512]{2,1,0:T(8,128)(2,1)}), bf16[8,768,512]{2,1,0:T(8,128)(2,1)}) %all-gather.6.cloned.1.call-update) | async-done | bytes 6291472 | tf_op jit(solution)/shard_map/all_gather | solution.py:45
  91.7 6.5 %copy.33 = bf16[4,2,96,8,512]{4,3,0,2,1:T(8,128)(2,1)} copy(bf16[4,2,96,8,512]{4,3,2,1,0:T(8,128)(2,1)} %bitcast.17) | data formatting | bytes 12582912 | tf_op jit(solution)/shard_map/reshape | solution.py:45
  (4 shorter events, 0.0 us)
Async XLA Ops:
  7.2 84.5 %all-gather.6.cloned.1.call-start = ((), (), s32[]{:S(2)}) async-start(), calls=%async_computation.1 | async-start | bytes 7864320 | tf_op jit(solution)/shard_map/all_gather | solution.py:45
  10.6 10.4 %copy-start = (f32[2,768,512]{2,1,0:T(8,128)}, f32[2,768,512]{2,1,0:T(8,128)S(1)}, u32[]{:S(2)}) copy-start(f32[2,768,512]{2,1,0:T(8,128)S(1)} %get-tuple-element.25) | copy-start | bytes 9437188
  19.5 1.5 %copy-start.1 = (f32[2,768]{1,0:T(2,128)}, f32[2,768]{1,0:T(2,128)S(1)}, u32[]{:S(2)}) copy-start(f32[2,768]{1,0:T(2,128)S(1)} %broadcast_multiply_fusion) | copy-start | bytes 18436
  19.5 1.5 %copy-start.2 = (f32[512,2]{0,1:T(2,128)S(1)}, f32[512,2]{0,1:T(2,128)}, u32[]{:S(2)}) copy-start(f32[512,2]{0,1:T(2,128)} %param.6) | copy-start | bytes 12292
  19.5 1.5 %copy-start.3 = (f32[512]{0:T(512)S(1)}, f32[512]{0:T(512)}, u32[]{:S(2)}) copy-start(f32[512]{0:T(512)} %param.7) | copy-start | bytes 6148
Sparse Core Ops, SparseCore 0:
  21.1 70.5 all-gather.5
